TPU v7x, 32 devices: a whole 2x2x4 slice. The times are simulated.
32 devices in a mesh: row: 4 (over y, x), col: 8 (over z, core).
Axes of the slice: x: 2, y: 2, z: 4, core: 2. Of those that a mesh axis runs over, the one named last changes fastest.
Arguments:
- pair: float32 [256, 256, 128], P('row', 'col'), may hold values from -6 to 6
- valid_length: int32 [1], replicated, may hold values from 64 to 255
- tri_in: bfloat16 [128, 512], replicated, may hold values from -0.5 to 0.5
- tri_gate: bfloat16 [128, 128], replicated, may hold values from -0.5 to 0.5
- tri_out: bfloat16 [128, 128], replicated, may hold values from -0.5 to 0.5
- att_in: bfloat16 [128, 512], replicated, may hold values from -16.9705627 to 16.9705627
- att_bias: bfloat16 [128, 4], replicated, may hold values from -0.5 to 0.5
- att_out: bfloat16 [128, 128], replicated, may hold values from -0.5 to 0.5
Outputs:
- pair_out: float32 [256, 256, 128], P('row', 'col')
Inputs may be any that keep to these rules, and one draw needn't show every extreme that they name: Tokens at positions below valid_length[0] are real, the rest are padding.
All inputs are finite; a program needn't handle non-finite values.
Results may differ from a plain program's by a relative error of at most 0.025.
Values may be sent and summed in bfloat16 or wider, within the bound.
No kernel may reach another device: no remote copies, remote signals or barrier semaphores. Data moves between devices by JAX's collectives and lax.ppermute only.
A program may use at most 128 MiB of HBM per device.

v0:
```python
import jax
import jax.numpy as jnp
from jax import lax
from jax.sharding import PartitionSpec as P


def layer_norm(values):
    center = values - jnp.mean(values, axis=-1, keepdims=True)
    return center * lax.rsqrt(jnp.mean(center * center, axis=-1, keepdims=True) + 1e-05)


def fold_keys(carry, keys_piece, values_piece, query_blocks, bias_heads, mask_bias):
    count = keys_piece.shape[1]
    nblocks, brows, cols_dev, heads, head_size = query_blocks.shape
    key_blocks = keys_piece.reshape(nblocks, brows, count, heads, head_size)
    value_blocks = values_piece.reshape(nblocks, brows, count, heads, head_size)

    def one_block(packed):
        query, keys, values, run_max, run_sum, accum = packed
        scores = jnp.einsum("ijhd,ikhd->ihjk", query, keys, preferred_element_type=jnp.float32)
        scores = scores + bias_heads[None] + mask_bias[None, None, None, :]
        new_max = jnp.maximum(run_max, jnp.max(scores, axis=-1))
        factor = jnp.exp(run_max - new_max)
        expo = jnp.exp(scores - new_max[..., None])
        new_sum = run_sum * factor + jnp.sum(expo, axis=-1)
        new_acc = accum * jnp.transpose(factor, (0, 2, 1))[..., None]
        new_acc = new_acc + jnp.einsum("ihjk,ikhd->ijhd", expo, values.astype(jnp.float32))
        return (new_max, new_sum, new_acc)

    return lax.map(one_block, (query_blocks, key_blocks, value_blocks) + tuple(carry))


def per_device(pair, valid_length, tri_in, tri_gate, tri_out, att_in, att_bias, att_out):
    rows_dev, cols_dev, width = pair.shape
    hidden = tri_out.shape[0]
    heads = att_bias.shape[1]
    head_size = width // heads
    total = cols_dev * lax.axis_size("col")
    row_start = lax.axis_index("row") * rows_dev
    col_start = lax.axis_index("col") * cols_dev
    tokens = jnp.arange(total)
    keep_all = (tokens < valid_length[0]).astype(jnp.float32)
    keep_rows = lax.dynamic_slice_in_dim(keep_all, row_start, rows_dev)
    keep_cols = lax.dynamic_slice_in_dim(keep_all, col_start, cols_dev)
    normed_pair = layer_norm(pair).astype(jnp.bfloat16)
    projected = jnp.dot(normed_pair, tri_in, preferred_element_type=jnp.float32)
    weight = (keep_rows[:, None] * keep_cols[None, :])[:, :, None]
    left_edges = (
        jax.nn.sigmoid(projected[..., :hidden]) * projected[..., hidden : 2 * hidden] * weight
    ).astype(jnp.bfloat16)
    right_edges = (
        jax.nn.sigmoid(projected[..., 2 * hidden : 3 * hidden])
        * projected[..., 3 * hidden :]
        * weight
    ).astype(jnp.bfloat16)
    right_rows = lax.all_gather(right_edges, "row", axis=0, tiled=True)
    swapped = lax.psum_scatter(
        jnp.einsum(
            "jkc,ikc->jic", right_rows, left_edges, preferred_element_type=jnp.float32
        ).astype(jnp.bfloat16),
        "col",
        scatter_dimension=0,
        tiled=True,
    ).astype(jnp.float32)
    normed_swapped = layer_norm(swapped).astype(jnp.bfloat16)
    tri_part = jnp.einsum(
        "jic,cd->ijd", normed_swapped, tri_out, preferred_element_type=jnp.float32
    )
    middle = (
        pair
        + jax.nn.sigmoid(jnp.dot(normed_pair, tri_gate, preferred_element_type=jnp.float32))
        * tri_part
    )
    normed_mid = layer_norm(middle).astype(jnp.bfloat16)
    bias_local = jnp.dot(normed_mid, att_bias, preferred_element_type=jnp.float32).astype(
        jnp.bfloat16
    )
    bias_rows = lax.all_gather(bias_local, "row", axis=0, tiled=True)
    bias_cols = lax.all_to_all(bias_rows, "col", split_axis=0, concat_axis=1, tiled=True)
    bias_heads = jnp.transpose(bias_cols.astype(jnp.float32), (2, 0, 1))
    mask_bias = jnp.where(tokens < valid_length[0], 0.0, -1000000000.0).astype(jnp.float32)
    nblocks = rows_dev // 8
    query = (
        jnp.dot(normed_mid, att_in[:, :width], preferred_element_type=jnp.float32)
        * head_size ** (-0.5)
    ).astype(jnp.bfloat16)
    query_blocks = query.reshape(nblocks, 8, cols_dev, heads, head_size)
    gate = jax.nn.sigmoid(
        jnp.dot(normed_mid, att_in[:, 3 * width :], preferred_element_type=jnp.float32)
    )
    start_state = (
        jnp.full((nblocks, 8, heads, cols_dev), -1e30, jnp.float32),
        jnp.zeros((nblocks, 8, heads, cols_dev), jnp.float32),
        jnp.zeros((nblocks, 8, cols_dev, heads, head_size), jnp.float32),
    )
    made = jnp.dot(
        lax.all_gather(normed_mid, "col", axis=1, tiled=True),
        att_in[:, width : 3 * width],
        preferred_element_type=jnp.float32,
    )
    keys_piece = made[..., :width].astype(jnp.bfloat16)
    values_piece = made[..., width:].astype(jnp.bfloat16)
    state = fold_keys(start_state, keys_piece, values_piece, query_blocks, bias_heads, mask_bias)
    run_sum = state[1]
    accum = state[2]
    attended = accum / jnp.transpose(run_sum, (0, 1, 3, 2))[..., None]
    attended = attended.reshape(rows_dev, cols_dev, width)
    gated = (gate * attended).astype(jnp.bfloat16)
    return middle + jnp.dot(gated, att_out, preferred_element_type=jnp.float32)


def solution(mesh):
    placed = (P("row", "col", None), P(), P(), P(), P(), P(), P(), P())
    return jax.shard_map(
        per_device, mesh=mesh, in_specs=placed, out_specs=P("row", "col", None), check_vma=False
    )
```

profile of v0, /device:TPU:0, one launch (start us, length us, event | category | flops | bytes accessed | tf_op | source)
XLA Modules:
  0.0 237.1 jit_solution(12051169796513153194)
XLA Ops:
  9.0 1.9 multiply_reduce_fusion.1
  10.9 2.1 fusion.40
  14.5 1.7 copy.17
  16.2 36.3 %all-gather.3.cloned.1.call-done = bf16[256,32,128]{2,1,0:T(8,128)(2,1)} async-done(((bf16[64,32,128]{2,1,0:T(8,128)(2,1)}), bf16[256,32,128]{2,1,0:T(8,128)(2,1)}) %all-gather.3.cloned.1.call-update) | async-done | bytes 2097168 | tf_op jit(solution)/shard_map/all_gather | solution.py:56
  52.5 3.9 %copy.18 = bf16[256,32,128]{0,1,2:T(8,128)(2,1)S(1)} copy(bf16[256,32,128]{2,1,0:T(8,128)(2,1)} %all-gather.3.cloned.1.call-done) | data formatting | bytes 4194304 | tf_op jit(solution)/shard_map/all_gather | solution.py:56
  56.4 3.3 %convert_bitcast_fusion = bf16[256,64,128]{0,1,2:T(8,128)(2,1)} fusion(bf16[64,32,128]{0,1,2:T(8,128)(2,1)S(1)} %copy.17, bf16[256,32,128]{0,1,2:T(8,128)(2,1)S(1)} %copy.18), kind=kOutput, calls=%fused_computation.24 | convolution fusion | flops 136314880 | bytes 6815744 | tf_op jit(solution)/shard_map/jkc,ikc->jic/dot_general | solution.py:58
  59.7 7.4 %copy.19 = bf16[256,64,128]{2,1,0:T(8,128)(2,1)} copy(bf16[256,64,128]{0,1,2:T(8,128)(2,1)} %convert_bitcast_fusion) | data formatting | bytes 8388608 | tf_op jit(solution)/shard_map/convert_element_type | solution.py:60
  67.1 50.0 %reduce-scatter.2.cloned.1.call-done = bf16[32,64,128]{2,1,0:T(8,128)(2,1)} async-done(((bf16[256,64,128]{2,1,0:T(8,128)(2,1)}), bf16[32,64,128]{2,1,0:T(8,128)(2,1)}) %reduce-scatter.2.cloned.1.call-update) | async-done | bytes 524304 | tf_op jit(solution)/shard_map/reduce_scatter | solution.py:57
  118.5 1.7 fusion.28
  120.2 1.6 fusion.29
  122.4 1.7 fusion.63
  126.2 1.8 convolution_convert_fusion.1
  128.1 9.1 %all_gather.11 = bf16[256,32,4]{1,2,0:T(4,128)(2,1)S(1)} all-gather(bf16[64,32,4]{1,2,0:T(4,128)(2,1)S(1)} %convolution_convert_fusion.1), channel_id=1, replica_groups=mesh['row'=4,'col'=8] {'row'}, dimensions={0}, use_global_device_ids=true | all-gather | bytes 81920 | tf_op jit(solution)/shard_map/all_gather | solution.py:78
  138.1 3.5 %all-to-all-start = ((bf16[8,2,2048]{2,1,0:T(2,128)(2,1)}), bf16[8,2,2048]{2,1,0:T(2,128)(2,1)S(1)}, u32[]{:S(2)}, u32[]{:S(2)}) async-start(bf16[8,2,2048]{2,1,0:T(2,128)(2,1)} %reshape.132), calls=%async_computation.1 | async-start | bytes 131072 | tf_op jit(solution)/shard_map/all_to_all | solution.py:79
  141.6 2.1 fusion.25
  143.7 3.1 %reshape.116 = bf16[8,8,32,4,32]{4,3,2,1,0:T(4,128)(2,1)S(1)} reshape(bf16[64,32,128]{2,1,0:T(8,128)(2,1)} %fusion.25) | data formatting | bytes 1048576 | tf_op jit(solution)/shard_map/reshape | solution.py:87
  146.9 2.2 all-to-all-done
  153.3 19.8 %all-gather.5.cloned.1.call-done = bf16[64,256,128]{2,1,0:T(8,128)(2,1)} async-done(((bf16[64,32,128]{2,1,0:T(8,128)(2,1)}), bf16[64,256,128]{2,1,0:T(8,128)(2,1)}) %all-gather.5.cloned.1.call-update) | async-done | bytes 4194320 | tf_op jit(solution)/shard_map/all_gather | solution.py:97
  173.1 4.6 %convolution_convert_fusion = bf16[64,256,256]{1,2,0:T(8,128)(2,1)S(1)} fusion(bf16[64,256,128]{2,1,0:T(8,128)(2,1)} %all-gather.5.cloned.1.call-done, bf16[128,512]{1,0:T(8,128)(2,1)} %param.15), kind=kOutput, calls=%fused_computation.23 | convolution fusion | flops 1077936128 | bytes 12648448 | tf_op jit(solution)/shard_map/dot_general | solution.py:96
  177.7 3.5 %fusion.62 = (bf16[64,256,128]{1,2,0:T(8,128)(2,1)}, bf16[64,256,128]{1,2,0:T(8,128)(2,1)}) fusion(bf16[64,256,256]{1,2,0:T(8,128)(2,1)S(1)} %convolution_convert_fusion), kind=kLoop, calls=%fused_computation.96 | loop fusion | bytes 16777216 | tf_op jit(solution)/shard_map/slice | solution.py:102
  181.2 39.1 %while.13 = (s32[]{:T(128)}, f32[8,8,4,32]{3,2,1,0:T(4,128)S(1)}, f32[8,8,32,4,32]{2,4,3,1,0:T(8,128)}, bf16[8,8,32,4,32]{4,3,2,1,0:T(4,128)(2,1)S(1)}, bf16[8,8...) while((s32[]{:T(128)}, f32[8,8,4,32]{3,2,1,0:T(4,128)S(1)}, ...), condition=%wide.region_10.11_spmd.clone, body=%wide.region_7.10_spmd.clone.sunk | while | flops 35165696 | bytes 5131381 | solution.py:30
  183.8 2.3 fusion.79
  188.8 2.3 fusion.79
  193.7 2.2 fusion.79
  198.6 2.2 fusion.79
  203.4 2.2 fusion.79
  208.3 2.2 fusion.79
  213.2 2.2 fusion.79
  218.1 2.2 fusion.79
  220.3 5.0 %broadcast_divide_fusion = f32[8,8,32,4,32]{2,4,3,1,0:T(8,128)} fusion(f32[8,8,32,4,32]{2,4,3,1,0:T(8,128)} %get-tuple-element.48, f32[8,8,32,4]{2,3,1,0:T(4,128)S(1)} %bitcast.104), kind=kLoop, calls=%fused_computation.25 | loop fusion | flops 262144 | bytes 2129920 | tf_op jit(solution)/shard_map/div | solution.py:106
  225.4 2.9 %copy.27 = f32[64,32,128]{2,1,0:T(8,128)S(1)} copy(f32[64,32,128]{1,2,0:T(8,128)} %bitcast.98) | data formatting | bytes 2097152 | tf_op jit(solution)/shard_map/reshape | solution.py:107
  228.2 2.3 convolution_add_fusion.1
  (91 shorter events, 33.3 us)
Async XLA Ops:
  6.5 4.4 %copy-start = (bf16[128,512]{1,0:T(8,128)(2,1)S(1)}, bf16[128,512]{1,0:T(8,128)(2,1)}, u32[]{:S(2)}) copy-start(bf16[128,512]{1,0:T(8,128)(2,1)} %param.12) | copy-start | bytes 393220
  6.5 45.9 %all-gather.3.cloned.1.call-start = ((), (), s32[]{:S(2)}) async-start(), calls=%async_computation.2 | async-start | bytes 2621440 | tf_op jit(solution)/shard_map/all_gather | solution.py:56
  14.4 102.7 %reduce-scatter.2.cloned.1.call-start = ((), (), s32[]{:S(2)}) async-start(), calls=%async_computation.3 | async-start | bytes 4718592 | tf_op jit(solution)/shard_map/reduce_scatter | solution.py:57
  67.1 54.9 %copy-start.3 = (bf16[128,128]{1,0:T(8,128)(2,1)S(1)}, bf16[128,128]{1,0:T(8,128)(2,1)}, u32[]{:S(2)}) copy-start(bf16[128,128]{1,0:T(8,128)(2,1)} %param.14) | copy-start | bytes 98308
  67.1 55.3 %copy-start.1 = (f32[64,32,128]{2,1,0:T(8,128)S(1)}, f32[64,32,128]{2,1,0:T(8,128)}, u32[]{:S(2)}) copy-start(f32[64,32,128]{2,1,0:T(8,128)} %param.10) | copy-start | bytes 3145732
  67.1 55.3 %copy-start.5 = (bf16[128,128]{1,0:T(8,128)(2,1)S(1)}, bf16[128,128]{1,0:T(8,128)(2,1)}, u32[]{:S(2)}) copy-start(bf16[128,128]{1,0:T(8,128)(2,1)} %param.13) | copy-start | bytes 98308
  67.1 106.0 %all-gather.5.cloned.1.call-start = ((), (), s32[]{:S(2)}) async-start(), calls=%async_computation.4 | async-start | bytes 4718592 | tf_op jit(solution)/shard_map/all_gather | solution.py:97
  122.3 3.9 %copy-start.4 = (bf16[128,4]{0,1:T(4,128)(2,1)S(1)}, bf16[128,4]{0,1:T(4,128)(2,1)}, u32[]{:S(2)}) copy-start(bf16[128,4]{0,1:T(4,128)(2,1)} %param.16) | copy-start | bytes 3076
  138.1 11.0 %all-to-all-start = ((bf16[8,2,2048]{2,1,0:T(2,128)(2,1)}), bf16[8,2,2048]{2,1,0:T(2,128)(2,1)S(1)}, u32[]{:S(2)}, u32[]{:S(2)}) async-start(bf16[8,2,2048]{2,1,0:T(2,128)(2,1)} %reshape.132), calls=%async_computation.1 | async-start | bytes 131072 | tf_op jit(solution)/shard_map/all_to_all | solution.py:79
  225.4 2.9 %copy-start.2 = (bf16[64,32,128]{2,1,0:T(8,128)(2,1)S(1)}, bf16[64,32,128]{2,1,0:T(8,128)(2,1)}, u32[]{:S(2)}) copy-start(bf16[64,32,128]{2,1,0:T(8,128)(2,1)} %multiply_convert_fusion) | copy-start | bytes 1572868
  225.4 2.9 %copy-start.6 = (bf16[128,128]{1,0:T(8,128)(2,1)S(1)}, bf16[128,128]{1,0:T(8,128)(2,1)}, u32[]{:S(2)}) copy-start(bf16[128,128]{1,0:T(8,128)(2,1)} %param.17) | copy-start | bytes 98308
Sparse Core Ops, SparseCore 0:
  14.5 37.8 all-gather.2
  67.2 49.8 reduce-scatter.1
  126.3 46.7 all-gather.4
where the time goes:
time: 239 us; the launch traced here: 237 us
  waiting for transfers between devices  108 us (45%)
  matrix products  47.5 us (20%)
  local copies, waits for them, and re-layouts  27.6 us (12%)
  other arithmetic  26.6 us (11%)
  between operations  14 us (6%)
  blocking collectives  9.12 us (4%)
  starting transfers between devices  3.61 us (2%)
    reduce_scatter x1, waiting for transfers between devices, per_device(): lax.psum_scatter(jnp.einsum('jkc,ikc->jic', right_rows, left_edges, prefe...  50 us
    all_gather x1, waiting for transfers between devices, per_device(): right_rows = lax.all_gather(right_edges, 'row', axis=0, tiled=True)  36.3 us
    all_gather x1, waiting for transfers between devices, per_device(): lax.all_gather(normed_mid, 'col', axis=1, tiled=True)  19.8 us
    dot_general x8, matrix products, one_block(): jnp.einsum('ihjk,ikhd->ijhd', expo, values.astype(jnp.float32))  17.9 us
    dot_general x8, matrix products, one_block(): jnp.einsum('ijhd,ikhd->ihjk', query, keys, preferred_element_type=jnp.flo...  11.3 us
    all_gather x1, blocking collectives, per_device(): bias_rows = lax.all_gather(bias_local, 'row', axis=0, tiled=True)  9.12 us
    convert_element_type x1, local copies, waits for them, and re-layouts, per_device(): swapped = lax.psum_scatter(jnp.einsum('jkc,ikc->jic', right_rows, left_ed...  7.38 us
    select_n x8, other arithmetic, per_device(): jnp.where(tokens < valid_length[0], 0.0, -1000000000.0).astype(jnp.float32)  5.17 us
  transfers between devices with their start and end apart: 4, of which 4 were waited for; matrix products, arithmetic and copies ran while one was open for 6% of the time, Pallas kernels for 0%

commit v1 on v0

--- a/solution.py
+++ b/solution.py
@@ -2,6 +2,20 @@
 import jax.numpy as jnp
 from jax import lax
 from jax.sharding import PartitionSpec as P
+
+
+def ring_apply(value, axis, dim, make, out_dim):
+    ways, here, lap = (lax.axis_size(axis), lax.axis_index(axis), value.shape[dim])
+    earlier, later = ([], [])
+    going_up = going_down = value
+    for far in range(ways // 2 + 1):
+        earlier.append(make(going_up, (here - far) % ways * lap))
+        if 0 < far < ways - ways // 2:
+            later.append(make(going_down, (here + far) % ways * lap))
+        going_up = lax.ppermute(going_up, axis, [(d, (d + 1) % ways) for d in range(ways)])
+        going_down = lax.ppermute(going_down, axis, [(d, (d - 1) % ways) for d in range(ways)])
+    line = jnp.concatenate([*earlier[::-1], *later], axis=out_dim)
+    return jnp.roll(line, (here - ways // 2) * earlier[0].shape[out_dim], axis=out_dim)
 
 
 def layer_norm(values):
@@ -53,10 +67,15 @@
         * projected[..., 3 * hidden :]
         * weight
     ).astype(jnp.bfloat16)
-    right_rows = lax.all_gather(right_edges, "row", axis=0, tiled=True)
     swapped = lax.psum_scatter(
-        jnp.einsum(
-            "jkc,ikc->jic", right_rows, left_edges, preferred_element_type=jnp.float32
+        ring_apply(
+            right_edges,
+            "row",
+            0,
+            lambda part, offset: jnp.einsum(
+                "jkc,ikc->jic", part, left_edges, preferred_element_type=jnp.float32
+            ),
+            0,
         ).astype(jnp.bfloat16),
         "col",
         scatter_dimension=0,

time: 239 us -> 268 us (1.12)
  local copies, waits for them, and re-layouts: 27.6 us -> 64.1 us
  waiting for transfers between devices: 108 us -> 87.5 us
  matrix products: 47.5 us -> 55 us
  starting transfers between devices: 3.61 us -> 8.61 us
    all_gather x1 -> x0, waiting for transfers between devices: 36.3 us -> none  [per_device(): right_rows = lax.all_gather(right_edges, 'row', axis=0, tiled=True)]
    concatenate x0 -> x1, local copies, waits for them, and re-layouts: none -> 19.4 us  [ring_apply(): jnp.roll(line, (here - ways // 2) * earlier[0].shape[out_dim], axis=out_dim)]
    ppermute x0 -> x3, waiting for transfers between devices: none -> 13.2 us  [the longest x1 6.98 us: ring_apply(): lax.ppermute(going_down, axis, [(d, (d - 1) % ways) for d in range(ways)])]
    ppermute x0 -> x3, local copies, waits for them, and re-layouts: none -> 11.1 us  [the longest x2 7.41 us: ring_apply(): lax.ppermute(going_up, axis, [(d, (d + 1) % ways) for d in range(ways)])]
    convert_element_type x1 -> x3, local copies, waits for them, and re-layouts: 7.38 us -> 18 us  [the longest x2 14.3 us: per_device(): swapped = lax.psum_scatter(ring_apply(right_edges, 'row', 0, lambda part,...]
    dot_general x1 -> x4, matrix products: 3.28 us -> 10.8 us  [per_device(): jnp.einsum('jkc,ikc->jic', part, left_edges, preferred_element_type=jnp.f...]
    ppermute x0 -> x3, starting transfers between devices: none -> 4.99 us  [the longest x2 4.02 us: ring_apply(): lax.ppermute(going_up, axis, [(d, (d + 1) % ways) for d in range(ways)])]
    all_gather x1 -> x0, local copies, waits for them, and re-layouts: 3.91 us -> none  [per_device(): right_rows = lax.all_gather(right_edges, 'row', axis=0, tiled=True)]
  transfers between devices with their start and end apart: 4 -> 6, of which waited for: 4 -> 6; matrix products, arithmetic and copies ran while one was open for 6% -> 12% of each run, Pallas kernels for 0% -> 0%
where the time goes in v1:
time: 268 us; the launch traced here: 265 us
  waiting for transfers between devices  87.5 us (33%)
  local copies, waits for them, and re-layouts  64.1 us (24%)
  matrix products  55 us (21%)
  other arithmetic  25.6 us (10%)
  between operations  14.4 us (5%)
  blocking collectives  9.12 us (3%)
  starting transfers between devices  8.61 us (3%)
    reduce_scatter x1, waiting for transfers between devices, per_device(): lax.psum_scatter(ring_apply(right_edges, 'row', 0, lambda part, offset: j...  50.3 us
    all_gather x1, waiting for transfers between devices, per_device(): lax.all_gather(normed_mid, 'col', axis=1, tiled=True)  21.4 us
    concatenate x1, local copies, waits for them, and re-layouts, ring_apply(): jnp.roll(line, (here - ways // 2) * earlier[0].shape[out_dim], axis=out_dim)  19.4 us
    dot_general x8, matrix products, one_block(): jnp.einsum('ihjk,ikhd->ijhd', expo, values.astype(jnp.float32))  17.9 us
    convert_element_type x2, local copies, waits for them, and re-layouts, per_device(): swapped = lax.psum_scatter(ring_apply(right_edges, 'row', 0, lambda part,...  14.3 us
    dot_general x8, matrix products, one_block(): jnp.einsum('ijhd,ikhd->ihjk', query, keys, preferred_element_type=jnp.flo...  11.3 us
    dot_general x4, matrix products, per_device(): jnp.einsum('jkc,ikc->jic', part, left_edges, preferred_element_type=jnp.f...  10.8 us
    all_gather x1, blocking collectives, per_device(): bias_rows = lax.all_gather(bias_local, 'row', axis=0, tiled=True)  9.12 us
  transfers between devices with their start and end apart: 6, of which 6 were waited for; matrix products, arithmetic and copies ran while one was open for 12% of the time, Pallas kernels for 0%

profile of v1, /device:TPU:0, one launch (start us, length us, event | category | flops | bytes accessed | tf_op | source)
XLA Modules:
  0.0 264.6 jit_solution(12739983495630724554)
XLA Ops:
  14.4 3.0 %collective-permute-start = (bf16[64,32,128]{2,1,0:T(8,128)(2,1)}, bf16[64,32,128]{2,1,0:T(8,128)(2,1)}, u32[]{:S(2)}, u32[]{:S(2)}) collective-permute-start(bf16[64,32,128]{2,1,0:T(8,128)(2,1)} %get-tuple-element.107), channel_id=1, source_target_pairs={{0,8},{8,16},{16,24},{24,0},{1,9},{9,17},{17,25},{25,1},{2,10},{10... | collective-permute-start | bytes 1572872 | tf_op jit(solution)/shard_map/ppermute | solution.py:15
  18.3 3.7 %copy.28 = bf16[64,32,128]{0,1,2:T(8,128)(2,1)} copy(bf16[64,32,128]{2,1,0:T(8,128)(2,1)} %get-tuple-element.107) | data formatting | bytes 1048576 | tf_op jit(solution)/shard_map/convert_element_type | solution.py:69
  25.7 5.7 %collective-permute-done = bf16[64,32,128]{2,1,0:T(8,128)(2,1)} collective-permute-done((bf16[64,32,128]{2,1,0:T(8,128)(2,1)}, bf16[64,32,128]{2,1,0:T(8,128)(2,1)}, u32[]{:S(2)}, u32[]{:S(2)}) %collective-permute-start) | collective-permute-done | bytes 524320 | tf_op jit(solution)/shard_map/ppermute | solution.py:15
  32.5 3.7 %copy.26 = bf16[64,32,128]{0,1,2:T(8,128)(2,1)} copy(bf16[64,32,128]{2,1,0:T(8,128)(2,1)} %collective-permute-done) | data formatting | bytes 1048576 | tf_op jit(solution)/shard_map/ppermute | solution.py:15
  36.2 7.0 %collective-permute-done.2 = bf16[64,32,128]{2,1,0:T(8,128)(2,1)} collective-permute-done((bf16[64,32,128]{2,1,0:T(8,128)(2,1)}, bf16[64,32,128]{2,1,0:T(8,128)(2,1)}, u32[]{:S(2)}, u32[]{:S(2)}) %collective-permute-start.2) | collective-permute-done | bytes 524320 | tf_op jit(solution)/shard_map/ppermute | solution.py:16
  43.2 3.7 %copy.30 = bf16[64,32,128]{0,1,2:T(8,128)(2,1)} copy(bf16[64,32,128]{2,1,0:T(8,128)(2,1)} %collective-permute-done.2) | data formatting | bytes 1048576 | tf_op jit(solution)/shard_map/ppermute | solution.py:16
  46.9 3.5 %convolution_bitcast_fusion.3 = bf16[64,64,128]{0,1,2:T(8,128)(2,1)} fusion(bf16[64,32,128]{0,1,2:T(8,128)(2,1)S(1)} %copy.23, bf16[64,32,128]{0,1,2:T(8,128)(2,1)} %copy.26), kind=kOutput, calls=%fused_computation.27 | convolution fusion | flops 33554432 | bytes 2097152 | tf_op jit(solution)/shard_map/jkc,ikc->jic/dot_general | solution.py:75
  53.0 3.7 %copy.24 = bf16[64,32,128]{0,1,2:T(8,128)(2,1)} copy(bf16[64,32,128]{2,1,0:T(8,128)(2,1)} %collective-permute-done.1) | data formatting | bytes 1048576 | tf_op jit(solution)/shard_map/ppermute | solution.py:15
  56.7 3.3 %convolution_bitcast_fusion.4 = bf16[64,64,128]{0,1,2:T(8,128)(2,1)} fusion(bf16[64,32,128]{0,1,2:T(8,128)(2,1)S(1)} %copy.23, bf16[64,32,128]{0,1,2:T(8,128)(2,1)} %copy.24), kind=kOutput, calls=%fused_computation.28 | convolution fusion | flops 33554432 | bytes 2097152 | tf_op jit(solution)/shard_map/jkc,ikc->jic/dot_general | solution.py:75
  60.0 19.4 %concatenate.6 = bf16[512,64,128]{0,1,2:T(8,128)(2,1)} concatenate(bf16[64,64,128]{0,1,2:T(8,128)(2,1)} %convolution_bitcast_fusion.4, bf16[64,64,128]{0,1,2:T(8,128)(2,1)} %convolution_bitcast_fusion.3, bf16[64,64,128]{0,1,2:T(8,128)(2,1)S(1)} %convolution_bitcast_fusion.2, bf16[64,64,128]{0,1,2:T(8,128)(2,1)} %convolution_bitcast_fusion.1, ...), dimensions={0} | concatenate | bytes 16777216 | tf_op jit(solution)/shard_map/jit(_roll_dynamic)/concatenate | solution.py:18
  79.4 7.0 %dynamic-slice_convert_fusion = bf16[256,64,128]{0,1,2:T(8,128)(2,1)} fusion(bf16[512,64,128]{0,1,2:T(8,128)(2,1)} %concatenate.6, s32[]{:T(128)S(6)} %select_n.26), kind=kLoop, calls=%fused_computation.23 | loop fusion | bytes 8388612 | tf_op jit(solution)/shard_map/convert_element_type | solution.py:79
  86.3 7.4 %copy.31 = bf16[256,64,128]{2,1,0:T(8,128)(2,1)} copy(bf16[256,64,128]{0,1,2:T(8,128)(2,1)} %dynamic-slice_convert_fusion) | data formatting | bytes 8388608 | tf_op jit(solution)/shard_map/convert_element_type | solution.py:79
  94.0 50.3 %reduce-scatter.2.cloned.1.call-done = bf16[32,64,128]{2,1,0:T(8,128)(2,1)} async-done(((bf16[256,64,128]{2,1,0:T(8,128)(2,1)}), bf16[32,64,128]{2,1,0:T(8,128)(2,1)}) %reduce-scatter.2.cloned.1.call-update) | async-done | bytes 524304 | tf_op jit(solution)/shard_map/reduce_scatter | solution.py:70
  155.3 9.1 %all_gather.7 = bf16[256,32,4]{1,2,0:T(4,128)(2,1)S(1)} all-gather(bf16[64,32,4]{1,2,0:T(4,128)(2,1)S(1)} %convolution_convert_fusion.1), channel_id=1, replica_groups=mesh['row'=4,'col'=8] {'row'}, dimensions={0}, use_global_device_ids=true | all-gather | bytes 81920 | tf_op jit(solution)/shard_map/all_gather | solution.py:97
  165.3 3.3 %all-to-all-start = ((bf16[8,2,2048]{2,1,0:T(2,128)(2,1)}), bf16[8,2,2048]{2,1,0:T(2,128)(2,1)S(1)}, u32[]{:S(2)}, u32[]{:S(2)}) async-start(bf16[8,2,2048]{2,1,0:T(2,128)(2,1)} %reshape.132), calls=%async_computation.1 | async-start | bytes 131072 | tf_op jit(solution)/shard_map/all_to_all | solution.py:98
  170.8 3.1 %reshape.116 = bf16[8,8,32,4,32]{4,3,2,1,0:T(4,128)(2,1)S(1)} reshape(bf16[64,32,128]{2,1,0:T(8,128)(2,1)} %fusion.25) | data formatting | bytes 1048576 | tf_op jit(solution)/shard_map/reshape | solution.py:106
  173.9 2.4 all-to-all-done
  178.8 21.4 %all-gather.2.cloned.1.call-done = bf16[64,256,128]{2,1,0:T(8,128)(2,1)} async-done(((bf16[64,32,128]{2,1,0:T(8,128)(2,1)}), bf16[64,256,128]{2,1,0:T(8,128)(2,1)}) %all-gather.2.cloned.1.call-update) | async-done | bytes 4194320 | tf_op jit(solution)/shard_map/all_gather | solution.py:116
  200.3 4.6 %convolution_convert_fusion = bf16[64,256,256]{1,2,0:T(8,128)(2,1)S(1)} fusion(bf16[64,256,128]{2,1,0:T(8,128)(2,1)} %all-gather.2.cloned.1.call-done, bf16[128,512]{1,0:T(8,128)(2,1)} %param.15), kind=kOutput, calls=%fused_computation.24 | convolution fusion | flops 1077936128 | bytes 12648448 | tf_op jit(solution)/shard_map/dot_general | solution.py:115
  204.9 3.5 %fusion.62 = (bf16[64,256,128]{1,2,0:T(8,128)(2,1)}, bf16[64,256,128]{1,2,0:T(8,128)(2,1)}) fusion(bf16[64,256,256]{1,2,0:T(8,128)(2,1)S(1)} %convolution_convert_fusion), kind=kLoop, calls=%fused_computation.100 | loop fusion | bytes 16777216 | tf_op jit(solution)/shard_map/slice | solution.py:121
  208.4 39.1 %while.13 = (s32[]{:T(128)}, f32[8,8,4,32]{3,2,1,0:T(4,128)S(1)}, f32[8,8,32,4,32]{2,4,3,1,0:T(8,128)}, bf16[8,8,32,4,32]{4,3,2,1,0:T(4,128)(2,1)S(1)}, bf16[8,8...) while((s32[]{:T(128)}, f32[8,8,4,32]{3,2,1,0:T(4,128)S(1)}, ...), condition=%wide.region_10.11_spmd.clone, body=%wide.region_7.10_spmd.clone.sunk | while | flops 35165696 | bytes 5131381 | solution.py:44
  211.0 2.3 fusion.85
  215.9 2.3 fusion.85
  220.9 2.2 fusion.85
  225.8 2.2 fusion.85
  230.6 2.3 fusion.85
  235.5 2.2 fusion.85
  240.4 2.2 fusion.85
  245.3 2.2 fusion.85
  247.5 5.0 %broadcast_divide_fusion = f32[8,8,32,4,32]{2,4,3,1,0:T(8,128)} fusion(f32[8,8,32,4,32]{2,4,3,1,0:T(8,128)} %get-tuple-element.48, f32[8,8,32,4]{2,3,1,0:T(4,128)S(1)} %bitcast.116), kind=kLoop, calls=%fused_computation.29 | loop fusion | flops 262144 | bytes 2129920 | tf_op jit(solution)/shard_map/div | solution.py:125
  252.6 2.9 %copy.39 = f32[64,32,128]{2,1,0:T(8,128)S(1)} copy(f32[64,32,128]{1,2,0:T(8,128)} %bitcast.110) | data formatting | bytes 2097152 | tf_op jit(solution)/shard_map/reshape | solution.py:126
  255.4 2.3 convolution_add_fusion.1
  (108 shorter events, 53.1 us)
Async XLA Ops:
  6.5 4.4 %copy-start = (bf16[128,512]{1,0:T(8,128)(2,1)S(1)}, bf16[128,512]{1,0:T(8,128)(2,1)}, u32[]{:S(2)}) copy-start(bf16[128,512]{1,0:T(8,128)(2,1)} %param.12) | copy-start | bytes 393220
  6.5 137.8 %reduce-scatter.2.cloned.1.call-start = ((), (), s32[]{:S(2)}) async-start(), calls=%async_computation.2 | async-start | bytes 4718592 | tf_op jit(solution)/shard_map/reduce_scatter | solution.py:70
  14.4 17.0 %collective-permute-start = (bf16[64,32,128]{2,1,0:T(8,128)(2,1)}, bf16[64,32,128]{2,1,0:T(8,128)(2,1)}, u32[]{:S(2)}, u32[]{:S(2)}) collective-permute-start(bf16[64,32,128]{2,1,0:T(8,128)(2,1)} %get-tuple-element.107), channel_id=1, source_target_pairs={{0,8},{8,16},{16,24},{24,0},{1,9},{9,17},{17,25},{25,1},{2,10},{10... | collective-permute-start | bytes 1572872 | tf_op jit(solution)/shard_map/ppermute | solution.py:15
  17.3 25.8 %collective-permute-start.2 = (bf16[64,32,128]{2,1,0:T(8,128)(2,1)}, bf16[64,32,128]{2,1,0:T(8,128)(2,1)}, u32[]{:S(2)}, u32[]{:S(2)}) collective-permute-start(bf16[64,32,128]{2,1,0:T(8,128)(2,1)} %get-tuple-element.107), channel_id=1, source_target_pairs={{0,24},{8,0},{16,8},{24,16},{1,25},{9,1},{17,9},{25,17},{2,26},{10... | collective-permute-start | bytes 1572872 | tf_op jit(solution)/shard_map/ppermute | solution.py:16
  31.4 21.6 %collective-permute-start.1 = (bf16[64,32,128]{2,1,0:T(8,128)(2,1)}, bf16[64,32,128]{2,1,0:T(8,128)(2,1)}, u32[]{:S(2)}, u32[]{:S(2)}) collective-permute-start(bf16[64,32,128]{2,1,0:T(8,128)(2,1)} %collective-permute-done), channel_id=1, source_target_pairs={{0,8},{8,16},{16,24},{24,0},{1,9},{9,17},{17,25},{25,1},{2,10},{10... | collective-permute-start | bytes 1572872 | tf_op jit(solution)/shard_map/ppermute | solution.py:15
  46.9 3.5 %copy-start.4 = (bf16[64,32,128]{0,1,2:T(8,128)(2,1)S(1)}, bf16[64,32,128]{0,1,2:T(8,128)(2,1)}, u32[]{:S(2)}) copy-start(bf16[64,32,128]{0,1,2:T(8,128)(2,1)} %copy.30) | copy-start | bytes 1572868
  93.7 55.4 %copy-start.6 = (bf16[128,128]{1,0:T(8,128)(2,1)S(1)}, bf16[128,128]{1,0:T(8,128)(2,1)}, u32[]{:S(2)}) copy-start(bf16[128,128]{1,0:T(8,128)(2,1)} %param.14) | copy-start | bytes 98308
  93.7 55.8 %copy-start.2 = (f32[64,32,128]{2,1,0:T(8,128)S(1)}, f32[64,32,128]{2,1,0:T(8,128)}, u32[]{:S(2)}) copy-start(f32[64,32,128]{2,1,0:T(8,128)} %param.10) | copy-start | bytes 3145732
  93.7 55.8 %copy-start.8 = (bf16[128,128]{1,0:T(8,128)(2,1)S(1)}, bf16[128,128]{1,0:T(8,128)(2,1)}, u32[]{:S(2)}) copy-start(bf16[128,128]{1,0:T(8,128)(2,1)} %param.13) | copy-start | bytes 98308
  93.7 106.6 %all-gather.2.cloned.1.call-start = ((), (), s32[]{:S(2)}) async-start(), calls=%async_computation.3 | async-start | bytes 4718592 | tf_op jit(solution)/shard_map/all_gather | solution.py:116
  149.6 3.9 %copy-start.7 = (bf16[128,4]{0,1:T(4,128)(2,1)S(1)}, bf16[128,4]{0,1:T(4,128)(2,1)}, u32[]{:S(2)}) copy-start(bf16[128,4]{0,1:T(4,128)(2,1)} %param.16) | copy-start | bytes 3076
  165.3 11.0 %all-to-all-start = ((bf16[8,2,2048]{2,1,0:T(2,128)(2,1)}), bf16[8,2,2048]{2,1,0:T(2,128)(2,1)S(1)}, u32[]{:S(2)}, u32[]{:S(2)}) async-start(bf16[8,2,2048]{2,1,0:T(2,128)(2,1)} %reshape.132), calls=%async_computation.1 | async-start | bytes 131072 | tf_op jit(solution)/shard_map/all_to_all | solution.py:98
  204.9 3.5 %copy-start.5 = (f32[8,8,4,32]{3,2,1,0:T(4,128)S(1)}, f32[8,8,4,32]{3,2,1,0:T(4,128)}, u32[]{:S(2)}) copy-start(f32[8,8,4,32]{3,2,1,0:T(4,128)} %custom-call) | copy-start | bytes 98308
  252.6 2.9 %copy-start.3 = (bf16[64,32,128]{2,1,0:T(8,128)(2,1)S(1)}, bf16[64,32,128]{2,1,0:T(8,128)(2,1)}, u32[]{:S(2)}) copy-start(bf16[64,32,128]{2,1,0:T(8,128)(2,1)} %multiply_convert_fusion) | copy-start | bytes 1572868
  252.6 2.9 %copy-start.9 = (bf16[128,128]{1,0:T(8,128)(2,1)S(1)}, bf16[128,128]{1,0:T(8,128)(2,1)}, u32[]{:S(2)}) copy-start(bf16[128,128]{1,0:T(8,128)(2,1)} %param.17) | copy-start | bytes 98308
  252.6 5.2 %copy-start.1 = (bf16[128,512]{1,0:T(8,128)(2,1)S(1)}, bf16[128,512]{1,0:T(8,128)(2,1)}, u32[]{:S(2)}) copy-start(bf16[128,512]{1,0:T(8,128)(2,1)} %param.12) | copy-start | bytes 393220
Sparse Core Ops, SparseCore 0:
  93.9 50.4 reduce-scatter.1
  153.5 46.7 all-gather.1
